TPU v7x, 32 devices: a whole 2x2x4 slice. The times are simulated.
32 devices in a mesh: groups: 2 (over y), batch: 8 (over z, x), mp: 2 (over core).
Axes of the slice: x: 2, y: 2, z: 4, core: 2. Of those that a mesh axis runs over, the one named last changes fastest.
Arguments:
- hidden: bfloat16 [32, 1280], P(('groups', 'batch')), parts along dimension 0, may hold values from -6 to 6
- token_qkv: bfloat16 [3, 32, 1280], P(None, ('groups', 'batch'), 'mp'), parts along dimension 1, may hold values from -6 to 6
- self_cache: bfloat16 [2, 32, 128, 1280], P(None, ('groups', 'batch'), None, 'mp'), parts along dimension 1, may hold values from -6 to 6
- cross_kv: bfloat16 [2, 32, 64, 1280], P(None, ('groups', 'batch'), None, 'mp'), parts along dimension 1, may hold values from -6 to 6
- cache_len: int32 [32], P(('groups', 'batch')), parts along dimension 0, may hold values from 1 to 127
- finished: int32 [32], P(('groups', 'batch')), parts along dimension 0, may hold values 0 or 1
- new_slot: int32 [32], P(('groups', 'batch')), parts along dimension 0, may hold values from 0 to 15, as said below
- out_proj: bfloat16 [1280, 1280], P('mp'), may hold values from -0.15625 to 0.15625
- ln_gain: float32 [1280], replicated, may hold values from 0.5 to 1.5
- ln_bias: float32 [1280], replicated, may hold values from -3 to 3
- query_proj: bfloat16 [1280, 1280], P(None, 'mp'), may hold values from -3 to 3
Outputs:
- moved_cache: bfloat16 [2, 32, 128, 1280], P(None, ('groups', 'batch'), None, 'mp'), parts along dimension 1
- moved_out: bfloat16 [32, 1280], P(('groups', 'batch'), 'mp'), parts along dimension 0
There are 2 independent parts, one for each index of `groups`. A program takes and returns all parts, laid end to end along the dimension named above; an argument that names none is the same for every part. Nothing has to cross between parts.
Inputs may be any that keep to these rules, and one draw needn't show every extreme that they name: A permutation of the spans' slots. Span c's new owner new_slot[c] // 2 lies within 3 devices of its present one c // 2, counting the device order as a loop; of one device's spans at most one moves by any given signed distance.
All inputs are finite; a program needn't handle non-finite values. No bound on the sum of `finished` on one device may be relied on, other than what follows from the above.
Results may differ from a plain program's by a relative error of at most 0.015.
Values may be sent and summed in bfloat16 or wider, within the bound.
A program may use at most 64 MiB of HBM per device.

v0:
```python
import functools

import jax
import jax.numpy as jnp
from jax import lax
from jax.experimental import pallas as pl
from jax.experimental.pallas import tpu as pltpu
from jax.sharding import PartitionSpec as P

HEAD_DIM = 64
REACH = 3
MESH = pl.DeviceIdType.MESH
DISTANCES = [3, -3, 2, -2, 1, -1]
ROWS = 16
LAG = 3
EARLY = 1
MIDDLE = 14
HOLD = 8


def attend(query, keys, values, length, own):
    slots, width = keys.shape
    heads = width // HEAD_DIM
    rows = -(-heads // 16) * 16
    row = lax.broadcasted_iota(jnp.int32, (rows, width), 0)
    column = lax.broadcasted_iota(jnp.int32, (rows, width), 1)
    low = row * HEAD_DIM
    mine = (column >= low) & (column < low + HEAD_DIM)
    spread = jnp.where(mine, query.astype(jnp.float32), 0.0)
    factor = HEAD_DIM ** (-0.5)
    scores = (
        lax.dot_general(
            spread.astype(jnp.bfloat16),
            keys,
            (((1,), (1,)), ((), ())),
            preferred_element_type=jnp.float32,
        )
        * factor
    )
    if length is not None:
        usable = lax.broadcasted_iota(jnp.int32, (rows, slots), 1) < length
        scores = jnp.where(usable, scores, -1e30)
    highest = jnp.max(scores, axis=-1, keepdims=True)
    if own is not None:
        new_key, new_value = own
        own_score = jnp.sum(spread * new_key.astype(jnp.float32), axis=-1, keepdims=True) * factor
        highest = jnp.maximum(highest, own_score)
    weight = jnp.exp(scores - highest)
    if length is not None:
        weight = jnp.where(usable, weight, 0.0)
    total = jnp.sum(weight, axis=-1, keepdims=True)
    if own is not None:
        own_weight = jnp.exp(own_score - highest)
        total = total + own_weight
    weight = (weight / total).astype(jnp.bfloat16)
    mixed = jnp.dot(weight, values, preferred_element_type=jnp.float32)
    if own is not None:
        own_weight = (own_weight / total).astype(jnp.bfloat16).astype(jnp.float32)
        mixed = mixed + own_weight * new_value.astype(jnp.float32)
    return jnp.sum(jnp.where(mine, mixed, 0.0), axis=0, keepdims=True)


def kernel(
    count,
    cores,
    cache_len,
    finished,
    new_slot,
    hidden,
    token_qkv,
    self_cache,
    ln_gain,
    ln_bias,
    cross_hbm,
    out_proj_hbm,
    query_proj_hbm,
    moved_cache,
    moved_out,
    cross,
    out_proj,
    query_proj,
    updated,
    parcel,
    arrived,
    mark,
    mark_in,
    line,
    line_in,
    part,
    part_in,
    load_sem,
    cache_sems,
    mark_sems,
    line_sems,
    part_sems,
):
    spans, width = hidden.shape
    slots, local = self_cache.shape[2:]
    me = lax.axis_index("batch")
    core = lax.axis_index("mp")
    loads = [
        pltpu.make_async_copy(source, target, load_sem.at[i])
        for i, (source, target) in enumerate(
            [(out_proj_hbm, out_proj), (query_proj_hbm, query_proj), (cross_hbm, cross)]
        )
    ]
    for load in loads:
        load.start()

    barrier = pltpu.get_barrier_semaphore()
    targets = [lax.rem(me + distance + count, count) for distance in DISTANCES]
    for target in targets:
        pl.semaphore_signal(barrier, inc=1, device_id={"batch": target}, device_id_type=MESH)
    others = [lax.rem(core + k, cores) for k in range(1, cores)]
    for other in others:
        pl.semaphore_signal(barrier, inc=1, device_id={"mp": other}, device_id_type=MESH)

    half = count // 2
    alive, offset, place = [], [], []
    for c in range(spans):
        slot = new_slot[c]
        owner = lax.div(slot, spans)
        offset.append(lax.rem(owner - me + half + count, count) - half)
        place.append(lax.rem(slot, spans))
        alive.append(jnp.where(finished[c] == 0, 1, 0))

    position = lax.broadcasted_iota(jnp.int32, (slots, local), 0)
    for c in range(spans):
        length = cache_len[c]
        older = jnp.where(position < length * alive[c], 1.0, 0.0).astype(jnp.bfloat16)
        fresh = jnp.where(position == jnp.where(alive[c] == 1, length, -1), 1.0, 0.0).astype(
            jnp.bfloat16
        )
        for a in range(2):
            updated[a, c] = self_cache[a, c] * older + token_qkv[1 + a, c : c + 1, :] * fresh

    def flag(value, shape):
        return jnp.full(shape, jnp.where(value, 1.0, 0.0), jnp.float32).astype(jnp.bfloat16)

    marker_row = lax.broadcasted_iota(jnp.int32, mark.shape[1:], 0)
    for i, distance in enumerate(DISTANCES):
        marker = jnp.zeros(mark.shape[1:], jnp.float32)
        for c in range(spans):
            at = jnp.where(offset[c] == distance, place[c], -1)
            marker = jnp.where(marker_row == at, 1.0, marker)
        mark[i] = marker.astype(jnp.bfloat16)

    def send(source, target, sems, i, distance):
        return pltpu.make_async_remote_copy(
            src_ref=source,
            dst_ref=target,
            send_sem=sems.at[0, i],
            recv_sem=sems.at[1, i],
            device_id={"batch": targets[i]},
            device_id_type=MESH,
        )

    pl.semaphore_wait(barrier, len(targets) + len(others))
    mark_copies, cache_copies = [], []
    for i, distance in enumerate(DISTANCES):
        copy = send(mark.at[i], mark_in.at[i], mark_sems, i, distance)
        copy.start()
        mark_copies.append(copy)
    for i, distance in enumerate(DISTANCES):
        for a in range(2):
            total = updated[a, 0] * flag(offset[0] == distance, (1, local))
            for c in range(1, spans):
                total = total + updated[a, c] * flag(offset[c] == distance, (1, local))
            parcel[i, a] = total
        copy = send(parcel.at[i], arrived.at[i], cache_sems, i, distance)
        copy.start()
        cache_copies.append(copy)

    for l in range(spans):
        for a in range(2):
            total = updated[a, 0] * flag((offset[0] == 0) & (place[0] == l), (1, local))
            for c in range(1, spans):
                keep = flag((offset[c] == 0) & (place[c] == l), (1, local))
                total = total + updated[a, c] * keep
            moved_cache[a, l] = total

    contexts = []
    for c in range(spans):
        query, key, value = (token_qkv[k, c : c + 1, :] for k in range(3))
        contexts.append(
            attend(query, self_cache[0, c], self_cache[1, c], cache_len[c], (key, value))
        )
    pad = part.shape[0] - spans
    context = jnp.concatenate(contexts + [jnp.zeros((pad, local), jnp.float32)], 0)
    context = context.astype(jnp.bfloat16)
    loads[0].wait()
    part[...] = jnp.dot(context, out_proj[...], preferred_element_type=jnp.float32)
    part_copies = []
    for k, other in enumerate(others):
        copy = pltpu.make_async_remote_copy(
            src_ref=part,
            dst_ref=part_in.at[k],
            send_sem=part_sems.at[0, k],
            recv_sem=part_sems.at[1, k],
            device_id={"mp": other},
            device_id_type=MESH,
        )
        copy.start()
        part_copies.append(copy)
    loads[1].wait()
    loads[2].wait()
    for copy in part_copies:
        copy.wait()
    summed = part[...]
    for k in range(len(others)):
        summed = summed + part_in[k]
    resid = hidden[...].astype(jnp.float32) + summed[:spans]
    centre = jnp.mean(resid, axis=-1, keepdims=True)
    spread = jnp.mean((resid - centre) ** 2, axis=-1, keepdims=True)
    gain = ln_gain[...].reshape(1, width)
    bias = ln_bias[...].reshape(1, width)
    normed = (resid - centre) * lax.rsqrt(spread + 1e-05) * gain + bias
    normed = jnp.concatenate([normed, jnp.zeros((pad, width), jnp.float32)], 0)
    query = jnp.dot(
        normed.astype(jnp.bfloat16), query_proj[...], preferred_element_type=jnp.float32
    ).astype(jnp.bfloat16).astype(jnp.float32)
    decoded = []
    for c in range(spans):
        mixed = attend(query[c : c + 1], cross[0, c], cross[1, c], None, None)
        decoded.append(mixed * jnp.where(alive[c] == 1, 1.0, 0.0))

    line_copies = []
    blank = jnp.zeros((line.shape[1] - 1, local), jnp.float32)
    for i, distance in enumerate(DISTANCES):
        row = jnp.zeros((1, local), jnp.float32)
        for c in range(spans):
            row = row + decoded[c] * jnp.where(offset[c] == distance, 1.0, 0.0)
        line[i] = jnp.concatenate([row, blank], 0).astype(jnp.bfloat16)
        copy = send(line.at[i], line_in.at[i], line_sems, i, distance)
        copy.start()
        line_copies.append(copy)

    rows = []
    for l in range(spans):
        row = jnp.zeros((1, local), jnp.float32)
        for c in range(spans):
            keep = (offset[c] == 0) & (place[c] == l)
            row = row + decoded[c] * jnp.where(keep, 1.0, 0.0)
        rows.append(row)
    for i in range(len(DISTANCES)):
        mark_copies[i].wait()
        cache_copies[i].wait()
        for l in range(spans):
            taken = mark_in[i, l : l + 1, :]
            for a in range(2):
                moved_cache[a, l] = moved_cache[a, l] + arrived[i, a] * taken
    for i in range(len(DISTANCES)):
        line_copies[i].wait()
        for l in range(spans):
            taken = mark_in[i, l : l + 1, :].astype(jnp.float32)
            rows[l] = rows[l] + line_in[i, 0:1, :].astype(jnp.float32) * taken
    moved_out[...] = jnp.concatenate(rows, 0).astype(jnp.bfloat16)


def relay_kernel(
    count,
    cores,
    cache_len_hbm,
    finished_hbm,
    new_slot_hbm,
    hidden_hbm,
    token_qkv_hbm,
    cache_hbm,
    ln_gain_hbm,
    ln_bias_hbm,
    cross_hbm,
    out_proj_hbm,
    query_proj_hbm,
    moved_cache,
    moved_out,
    cache_len,
    finished,
    new_slot,
    hidden,
    token_qkv,
    ln_gain,
    ln_bias,
    self_cache,
    cross,
    out_proj,
    query_proj,
    own,
    raw_in,
    cross_out,
    cross_in,
    kept,
    final_out,
    final_in,
    final_far,
    pick,
    label,
    label_in,
    line,
    line_in,
    line_kept,
    line_out,
    line_cross,
    line_last,
    line_final,
    part,
    part_in,
    load_sem,
    raw_send,
    raw_recv,
    hop_sems,
    label_send,
    label_recv,
    line_send,
    line_recv,
    line_hops,
    part_sems,
):
    spans, width = hidden.shape
    slots, local = self_cache.shape[2:]
    steps, _, rows_per, _ = own.shape
    per = steps // 2
    me = lax.axis_index("batch")
    core = lax.axis_index("mp")
    level, column = lax.div(me, 2), lax.rem(me, 2)
    inner = (level == 1) | (level == REACH - 1)
    outer = jnp.logical_not(inner)
    barrier = pltpu.get_barrier_semaphore()

    def greet(where):
        pl.semaphore_signal(barrier, inc=1, device_id=where, device_id_type=MESH)

    mate_level = jnp.where(level == 0, 1, jnp.where(level == 1, 0, jnp.where(level == 2, 3, 2)))
    mate = mate_level * 2 + column
    mate_aside = mate_level * 2 + 1 - column
    aside = level * 2 + 1 - column
    across = (REACH - level) * 2 + column
    beyond = (REACH - mate_level) * 2 + column
    others = [lax.rem(core + k, cores) for k in range(1, cores)]
    for node in (mate, mate_aside, beyond):
        greet({"batch": node})

    @pl.when(inner)
    def _():
        greet({"batch": aside})
        greet({"batch": across})

    for other in others:
        greet({"mp": other})
    loads = [
        pltpu.make_async_copy(source, target, load_sem.at[i])
        for i, (source, target) in enumerate(
            [
                (out_proj_hbm, out_proj),
                (query_proj_hbm, query_proj),
                (cross_hbm, cross),
                (cache_hbm.at[0], self_cache.at[0]),
                (cache_hbm.at[1], self_cache.at[1]),
                (cache_len_hbm, cache_len),
                (finished_hbm, finished),
                (new_slot_hbm, new_slot),
                (hidden_hbm, hidden),
                (token_qkv_hbm, token_qkv),
                (ln_gain_hbm, ln_gain),
                (ln_bias_hbm, ln_bias),
            ]
        )
    ]
    for i in [3, *range(5, len(loads)), 4, 0, 1, 2]:
        loads[i].start()
    for load in loads[5:]:
        load.wait()

    alive = [jnp.where(finished[c] == 0, 1, 0) for c in range(spans)]

    def to(node, source, target, sent, received):
        return pltpu.make_async_remote_copy(
            src_ref=source,
            dst_ref=target,
            send_sem=sent,
            recv_sem=received,
            device_id={"batch": node},
            device_id_type=MESH,
        )

    def raw_copy(node, lane, way, k):
        return to(node, own.at[k], raw_in.at[way, k], raw_send.at[lane, k], raw_recv.at[way, k])

    def far_copy(k):
        return to(
            beyond,
            cross_out.at[k, pl.ds(spans, spans)],
            final_far.at[k],
            hop_sems.at[0, k],
            hop_sems.at[1, k],
        )

    def cross_copy(k):
        return to(
            across,
            cross_out.at[k, pl.ds(0, spans)],
            cross_in.at[k],
            hop_sems.at[2, k],
            hop_sems.at[3, k],
        )

    def final_copy(k):
        return to(mate, final_out.at[k], final_in.at[k], hop_sems.at[4, k], hop_sems.at[5, k])

    def label_copy(node, lane, way):
        return to(node, label, label_in.at[way], label_send.at[lane], label_recv.at[way])

    def line_copy(node, lane, way):
        return to(node, line, line_in.at[way], line_send.at[lane], line_recv.at[way])

    def line_cross_copy():
        return to(across, line_out, line_cross, line_hops.at[0], line_hops.at[1])

    def line_final_copy():
        return to(mate, line_last, line_final, line_hops.at[2], line_hops.at[3])

    label_row = lax.broadcasted_iota(jnp.int32, label.shape, 0)
    labels = jnp.zeros(label.shape, jnp.int32)
    for c in range(spans):
        labels = jnp.where(label_row == c, new_slot[c], labels)
    label[...] = labels.astype(jnp.float32)

    @pl.when(inner)
    def _():
        pl.semaphore_wait(barrier, 5 + len(others))

    @pl.when(outer)
    def _():
        pl.semaphore_wait(barrier, 3 + len(others))

    position = lax.broadcasted_iota(jnp.int32, (rows_per, local), 0)
    ends = [cache_len[c] * alive[c] for c in range(spans)]
    fresh_at = [jnp.where(alive[c] == 1, cache_len[c], -1) for c in range(spans)]

    def grow(k, _):
        a, r = lax.div(k, per), lax.rem(k, per)
        start = pl.multiple_of(r * rows_per, rows_per)
        at = position + start
        for c in range(spans):
            older = jnp.where(at < ends[c], 1.0, 0.0).astype(jnp.bfloat16)
            fresh = jnp.where(at == fresh_at[c], 1.0, 0.0).astype(jnp.bfloat16)
            new = jnp.where(a == 0, token_qkv[1, c : c + 1, :].astype(jnp.float32),
                            token_qkv[2, c : c + 1, :].astype(jnp.float32)).astype(jnp.bfloat16)
            own[k, c] = self_cache[a, c, pl.ds(start, rows_per), :] * older + new * fresh

        return 0

    def pass_on(k, _):
        @pl.when(outer)
        def _():
            raw_copy(mate, 0, 0, k).start()
            raw_copy(mate_aside, 1, 1, k).start()

        @pl.when(inner)
        def _():
            raw_copy(aside, 0, 2, k).start()

        return 0

    def grow_and_pass(k, _):
        grow(k, 0)
        pass_on(k, 0)
        return 0

    @pl.when(outer)
    def _():
        label_copy(mate, 0, 0).start()
        label_copy(mate_aside, 1, 1).start()

    @pl.when(inner)
    def _():
        label_copy(aside, 0, 2).start()

    loads[3].wait()
    lax.fori_loop(0, per, grow_and_pass, 0)
    loads[4].wait()
    lax.fori_loop(per, HOLD, grow_and_pass, 0)
    lax.fori_loop(HOLD, steps, grow, 0)

    def self_part():
        contexts = []
        for c in range(spans):
            query, key, value = (token_qkv[k, c : c + 1, :] for k in range(3))
            contexts.append(
                attend(query, self_cache[0, c], self_cache[1, c], cache_len[c], (key, value))
            )
        context = jnp.concatenate(contexts + [jnp.zeros((pad, local), jnp.float32)], 0)
        context = context.astype(jnp.bfloat16)
        loads[0].wait()
        part[...] = jnp.dot(context, out_proj[...], preferred_element_type=jnp.float32)

    def part_copy(k):
        return pltpu.make_async_remote_copy(
            src_ref=part,
            dst_ref=part_in.at[k],
            send_sem=part_sems.at[0, k],
            recv_sem=part_sems.at[1, k],
            device_id={"mp": others[k]},
            device_id_type=MESH,
        )

    pad = part.shape[0] - spans
    self_part()
    for k in range(len(others)):
        part_copy(k).start()

    @pl.when(inner)
    def _():
        for way in range(3):
            label_copy(mate, 0, way).wait_recv()
        sources = [label] + [label_in.at[way] for way in range(3)]
        nodes = [me, mate, across, beyond]
        for s, source in enumerate(sources):
            for c in range(spans):
                held = jnp.broadcast_to(source[c : c + 1, 0:1], (rows_per, local))
                for d, node in enumerate(nodes):
                    for l in range(spans):
                        wanted = jnp.full((rows_per, local), node * spans + l, jnp.int32)
                        pick[s * spans + c, d * spans + l] = jnp.where(
                            held == wanted.astype(jnp.float32), 1.0, 0.0
                        ).astype(jnp.bfloat16)

    def merge(k, _):
        for way in range(3):
            raw_copy(mate, 0, way, k).wait_recv()
        blocks = [own[k, c] for c in range(spans)]
        for way in range(3):
            blocks += [raw_in[way, k, c] for c in range(spans)]

        def gathered(d):
            total = blocks[0] * pick[0, d]
            for s in range(1, len(blocks)):
                total = total + blocks[s] * pick[s, d]
            return total

        for d in range(spans, 2 * spans):
            cross_out[k, d] = gathered(2 * spans + d)
        far_copy(k).start()
        for d in range(spans):
            cross_out[k, d] = gathered(2 * spans + d)
        cross_copy(k).start()
        for d in range(spans):
            final_out[k, d] = gathered(spans + d)
        final_copy(k).start()
        for d in range(spans):
            kept[k, d] = gathered(d)
        return 0

    def finish(k, _):
        cross_copy(k).wait_recv()
        a, r = lax.div(k, per), lax.rem(k, per)
        start = pl.multiple_of(r * rows_per, rows_per)
        for l in range(spans):
            moved_cache[a, l, pl.ds(start, rows_per), :] = kept[k, l] + cross_in[k, l]
        return 0

    def both(k, _):
        merge(k, 0)
        finish(k - LAG, 0)
        return 0

    @pl.when(inner)
    def _():
        lax.fori_loop(0, EARLY, merge, 0)

    loads[1].wait()
    loads[2].wait()
    for k in range(len(others)):
        part_copy(k).wait()
    summed = part[...]
    for k in range(len(others)):
        summed = summed + part_in[k]
    resid = hidden[...].astype(jnp.float32) + summed[:spans]
    centre = jnp.mean(resid, axis=-1, keepdims=True)
    spread = jnp.mean((resid - centre) ** 2, axis=-1, keepdims=True)
    gain = ln_gain[...].reshape(1, width)
    bias = ln_bias[...].reshape(1, width)
    normed = (resid - centre) * lax.rsqrt(spread + 1e-05) * gain + bias
    normed = jnp.concatenate([normed, jnp.zeros((pad, width), jnp.float32)], 0)
    query = jnp.dot(
        normed.astype(jnp.bfloat16), query_proj[...], preferred_element_type=jnp.float32
    ).astype(jnp.bfloat16).astype(jnp.float32)

    @pl.when(inner)
    def _():
        lax.fori_loop(EARLY, LAG, merge, 0)

    decoded = []
    for c in range(spans):
        mixed = attend(query[c : c + 1], cross[0, c], cross[1, c], None, None)
        decoded.append(mixed * jnp.where(alive[c] == 1, 1.0, 0.0))

    line[...] = jnp.concatenate(decoded, 0).astype(jnp.bfloat16)

    @pl.when(outer)
    def _():
        line_copy(mate, 0, 0).start()
        line_copy(mate_aside, 1, 1).start()

    @pl.when(inner)
    def _():
        line_copy(aside, 0, 2).start()

    lax.fori_loop(HOLD, steps, pass_on, 0)

    @pl.when(inner)
    def _():
        lax.fori_loop(LAG, MIDDLE, both, 0)
        for way in range(3):
            line_copy(mate, 0, way).wait_recv()
        blocks = []
        for held in [line] + [line_in.at[way] for way in range(3)]:
            blocks += [held[c : c + 1, :].astype(jnp.float32) for c in range(spans)]
        rows = []
        for d in range(4 * spans):
            total = blocks[0] * pick[0, d, 0:1, :].astype(jnp.float32)
            for s in range(1, len(blocks)):
                total = total + blocks[s] * pick[s, d, 0:1, :].astype(jnp.float32)
            rows.append(total)
        line_out[...] = jnp.concatenate(rows[2 * spans :], 0).astype(jnp.bfloat16)
        line_cross_copy().start()
        line_kept[...] = jnp.concatenate(rows[: 2 * spans], 0)
        lax.fori_loop(MIDDLE, steps, both, 0)
        line_cross_copy().wait_recv()
        total = line_kept[...] + line_cross[...].astype(jnp.float32)
        line_last[...] = total[spans:].astype(jnp.bfloat16)
        line_final_copy().start()
        moved_out[...] = total[:spans].astype(jnp.bfloat16)

    def land(k, _):
        final_copy(k).wait_recv()
        far_copy(k).wait_recv()
        a, r = lax.div(k, per), lax.rem(k, per)
        start = pl.multiple_of(r * rows_per, rows_per)
        for l in range(spans):
            moved_cache[a, l, pl.ds(start, rows_per), :] = final_in[k, l] + final_far[k, l]
        return 0

    def outer_sent(k, _):
        raw_copy(mate, 0, 0, k).wait_send()
        raw_copy(mate_aside, 1, 1, k).wait_send()
        return 0

    def inner_sent(k, _):
        raw_copy(aside, 0, 2, k).wait_send()
        far_copy(k).wait_send()
        cross_copy(k).wait_send()
        final_copy(k).wait_send()
        return 0

    @pl.when(inner)
    def _():
        lax.fori_loop(steps - LAG, steps, finish, 0)
        label_copy(aside, 0, 2).wait_send()
        line_copy(aside, 0, 2).wait_send()
        line_cross_copy().wait_send()
        line_final_copy().wait_send()
        lax.fori_loop(0, steps, inner_sent, 0)

    @pl.when(outer)
    def _():
        lax.fori_loop(0, steps, land, 0)
        label_copy(mate, 0, 0).wait_send()
        label_copy(mate_aside, 1, 1).wait_send()
        line_copy(mate, 0, 0).wait_send()
        line_copy(mate_aside, 1, 1).wait_send()
        line_final_copy().wait_recv()
        moved_out[...] = line_final[...]
        lax.fori_loop(0, steps, outer_sent, 0)


def body(
    hidden,
    token_qkv,
    self_cache,
    cross_kv,
    cache_len,
    finished,
    new_slot,
    out_proj,
    ln_gain,
    ln_bias,
    query_proj,
):
    count, cores = lax.axis_size("batch"), lax.axis_size("mp")
    spans, width = hidden.shape
    slots, local = self_cache.shape[2:]
    moves = len(DISTANCES)
    smem = pl.BlockSpec(memory_space=pltpu.SMEM)
    vmem = pl.BlockSpec(memory_space=pltpu.VMEM)
    away = pl.BlockSpec(memory_space=pl.ANY)
    bf16, f32 = jnp.bfloat16, jnp.float32
    operands = (
        cache_len,
        finished,
        new_slot,
        hidden,
        token_qkv,
        self_cache,
        ln_gain,
        ln_bias,
        cross_kv,
        out_proj,
        query_proj,
    )
    parcels = pltpu.VMEM((moves, 2, slots, local), bf16)
    tiles = pltpu.VMEM((moves, 16, local), bf16)
    dma = pltpu.SemaphoreType.DMA
    inputs = [pltpu.VMEM(array.shape, bf16) for array in (cross_kv, out_proj, query_proj)]
    parts = [pltpu.VMEM((8, width), f32), pltpu.VMEM((cores - 1, 8, width), f32)]
    steps = 2 * slots // ROWS
    if count == 2 * (REACH + 1):
        function, specs = relay_kernel, [away] * 8

        def blocks(*lead):
            return pltpu.VMEM(lead + (ROWS, local), bf16)

        small = [pltpu.SMEM((spans,), jnp.int32)] * 3 + [
            pltpu.VMEM(hidden.shape, bf16),
            pltpu.VMEM(token_qkv.shape, bf16),
            pltpu.VMEM(ln_gain.shape, f32),
            pltpu.VMEM(ln_bias.shape, f32),
        ]
        scratch = small + [pltpu.VMEM(self_cache.shape, bf16)] + inputs + [
            blocks(steps, spans),
            blocks(3, steps, spans),
            blocks(steps, 2 * spans),
            blocks(steps, spans),
            blocks(steps, spans),
            blocks(steps, spans),
            blocks(steps, spans),
            blocks(steps, spans),
            blocks(4 * spans, 4 * spans),
            pltpu.VMEM((8, 128), f32),
            pltpu.VMEM((3, 8, 128), f32),
            pltpu.VMEM((spans, local), bf16),
            pltpu.VMEM((3, spans, local), bf16),
            pltpu.VMEM((2 * spans, local), f32),
            pltpu.VMEM((2 * spans, local), bf16),
            pltpu.VMEM((2 * spans, local), bf16),
            pltpu.VMEM((spans, local), bf16),
            pltpu.VMEM((spans, local), bf16),
            *parts,
            dma((12,)),
            dma((2, steps)),
            dma((3, steps)),
            dma((6, steps)),
            dma((2,)),
            dma((3,)),
            dma((2,)),
            dma((3,)),
            dma((4,)),
            dma((2, cores - 1)),
        ]
    else:
        function, specs = kernel, [smem] * 3 + [vmem] * 5
        scratch = inputs + [
            pltpu.VMEM(self_cache.shape, bf16),
            parcels,
            parcels,
            tiles,
            tiles,
            tiles,
            tiles,
            *parts,
            dma((3,)),
            dma((2, moves)),
            dma((2, moves)),
            dma((2, moves)),
            dma((2, cores - 1)),
        ]
    return pl.pallas_call(
        functools.partial(function, count, cores),
        out_shape=(
            pltpu.VMEM(self_cache.shape, bf16),
            pltpu.VMEM((spans, local), bf16),
        ),
        in_specs=specs + [away] * 3,
        out_specs=(vmem, vmem),
        scratch_shapes=scratch,
        compiler_params=pltpu.CompilerParams(collective_id=0, has_side_effects=True),
    )(*operands)


def solution(mesh):
    placed = (
        P(("groups", "batch"), None),
        P(None, ("groups", "batch"), "mp"),
        P(None, ("groups", "batch"), None, "mp"),
        P(None, ("groups", "batch"), None, "mp"),
        P(("groups", "batch")),
        P(("groups", "batch")),
        P(("groups", "batch")),
        P("mp", None),
        P(),
        P(),
        P(None, "mp"),
    )
    return jax.shard_map(
        body,
        mesh=mesh,
        in_specs=placed,
        out_specs=(P(None, ("groups", "batch"), None, "mp"), P(("groups", "batch"), "mp")),
        check_vma=False,
    )
```

profile of v0, /device:TPU:0, one launch (start us, length us, event | category | flops | bytes accessed | tf_op | source)
XLA Modules:
  0.0 43.0 jit_solution(14119705166254605033)
XLA Ops:
  0.6 40.9 %shard_map.122 = (bf16[2,2,128,640]{3,2,1,0:T(8,128)(2,1)S(1)}, bf16[2,640]{1,0:T(2,128)(2,1)S(1)}) custom-call(s32[2]{0:T(128)} %cache_len_hbm.1, s32[2]{0:T(128)} %finished_hbm.1, s32[2]{0:T(128)} %new_slot_hbm.1, bf16[2,1280]{1,0:T(2,128)(2,1)} %hidden_hbm.1, bf16[3,2,640]{2,1,0:T(2,128)(2,1)} %token_qkv_hbm.1, bf16[2,2,128,640]{3,2,1,0:T(8,128)(2,1)} %cache_hbm.1, ...), custom_call_target="tpu_custom_call" | custom-call | tf_op jit(solution)/shard_map/pallas_call | solution.py:776
  41.6 0.8 %copy.15 = bf16[2,2,128,640]{3,2,1,0:T(8,128)(2,1)} copy(bf16[2,2,128,640]{3,2,1,0:T(8,128)(2,1)S(1)} %get-tuple-element.2) | data formatting | bytes 1310720
  42.4 0.6 %copy.16 = bf16[2,640]{1,0:T(2,128)(2,1)} copy(bf16[2,640]{1,0:T(2,128)(2,1)S(1)} %get-tuple-element.3) | data formatting | bytes 5120
where the time goes:
time: 43.1 us; the launch traced here: 43 us
  Pallas kernels  40.9 us (95%)
  local copies, waits for them, and re-layouts  1.42 us (3%)
  between operations  0.64 us (1%)
    pallas_call x1, Pallas kernels, body(): pl.pallas_call(functools.partial(function, count, cores), out_shape=(pltp...  40.9 us
    unnamed x2, local copies, waits for them, and re-layouts  1.42 us

commit v1 on v0

--- a/solution.py
+++ b/solution.py
@@ -12,10 +12,12 @@
 MESH = pl.DeviceIdType.MESH
 DISTANCES = [3, -3, 2, -2, 1, -1]
 ROWS = 16
+WHOLE = 6
+JOINED = 14
+AHEAD = 5
 LAG = 3
-EARLY = 1
-MIDDLE = 14
-HOLD = 8
+BEHIND = 3
+LINES = 11
 
 
 def attend(query, keys, values, length, own):
@@ -314,6 +316,7 @@
     line_recv,
     line_hops,
     part_sems,
+    pass_sems,
 ):
     spans, width = hidden.shape
     slots, local = self_cache.shape[2:]
@@ -336,12 +339,11 @@
     across = (REACH - level) * 2 + column
     beyond = (REACH - mate_level) * 2 + column
     others = [lax.rem(core + k, cores) for k in range(1, cores)]
-    for node in (mate, mate_aside, beyond):
+    for node in (mate, beyond, aside):
         greet({"batch": node})
 
     @pl.when(inner)
     def _():
-        greet({"batch": aside})
         greet({"batch": across})
 
     for other in others:
@@ -385,6 +387,12 @@
     def raw_copy(node, lane, way, k):
         return to(node, own.at[k], raw_in.at[way, k], raw_send.at[lane, k], raw_recv.at[way, k])
 
+    def pass_copy(k):
+        return to(across, raw_in.at[0, k], raw_in.at[2, k], pass_sems.at[k], raw_recv.at[2, k])
+
+    def outer_pass_copy(k):
+        return to(mate, raw_in.at[1, k], raw_in.at[1, k], pass_sems.at[k], raw_recv.at[1, k])
+
     def far_copy(k):
         return to(
             beyond,
@@ -394,11 +402,23 @@
             hop_sems.at[1, k],
         )
 
-    def cross_copy(k):
+    def turn_copy(k):
         return to(
-            across,
-            cross_out.at[k, pl.ds(0, spans)],
-            cross_in.at[k],
+            mate,
+            cross_out.at[k, pl.ds(spans, spans)],
+            raw_in.at[2, k],
+            hop_sems.at[0, k],
+            raw_recv.at[2, k],
+        )
+
+    def turned_copy(k):
+        return to(aside, raw_in.at[2, k], final_far.at[k], pass_sems.at[k], hop_sems.at[1, k])
+
+    def cross_copy(k, node, count):
+        return to(
+            node,
+            cross_out.at[k, pl.ds(0, count)],
+            cross_in.at[k, pl.ds(0, count)],
             hop_sems.at[2, k],
             hop_sems.at[3, k],
         )
@@ -411,6 +431,12 @@
 
     def line_copy(node, lane, way):
         return to(node, line, line_in.at[way], line_send.at[lane], line_recv.at[way])
+
+    def label_pass_copy(node, here, there):
+        return to(node, label_in.at[here], label_in.at[there], label_send.at[2], label_recv.at[there])
+
+    def line_pass_copy():
+        return to(mate, line_in.at[1], line_in.at[1], line_send.at[2], line_recv.at[1])
 
     def line_cross_copy():
         return to(across, line_out, line_cross, line_hops.at[0], line_hops.at[1])
@@ -426,7 +452,7 @@
 
     @pl.when(inner)
     def _():
-        pl.semaphore_wait(barrier, 5 + len(others))
+        pl.semaphore_wait(barrier, 4 + len(others))
 
     @pl.when(outer)
     def _():
@@ -449,11 +475,23 @@
 
         return 0
 
+    def pass_whole(k, _):
+        grow(k, 0)
+
+        @pl.when(outer)
+        def _():
+            raw_copy(mate, 0, 0, k).start()
+
+        @pl.when(inner)
+        def _():
+            raw_copy(across, 0, 1, k).start()
+
+        return 0
+
     def pass_on(k, _):
         @pl.when(outer)
         def _():
-            raw_copy(mate, 0, 0, k).start()
-            raw_copy(mate_aside, 1, 1, k).start()
+            raw_copy(aside, 1, 1, k).start()
 
         @pl.when(inner)
         def _():
@@ -461,25 +499,30 @@
 
         return 0
 
-    def grow_and_pass(k, _):
-        grow(k, 0)
-        pass_on(k, 0)
-        return 0
-
     @pl.when(outer)
     def _():
         label_copy(mate, 0, 0).start()
-        label_copy(mate_aside, 1, 1).start()
+        label_copy(aside, 1, 1).start()
 
     @pl.when(inner)
     def _():
         label_copy(aside, 0, 2).start()
+        label_copy(across, 1, 3).start()
 
     loads[3].wait()
-    lax.fori_loop(0, per, grow_and_pass, 0)
+    lax.fori_loop(0, WHOLE, pass_whole, 0)
+    lax.fori_loop(WHOLE, per, grow, 0)
     loads[4].wait()
-    lax.fori_loop(per, HOLD, grow_and_pass, 0)
-    lax.fori_loop(HOLD, steps, grow, 0)
+    lax.fori_loop(per, steps, grow, 0)
+
+    @pl.when(inner)
+    def _():
+        lax.fori_loop(WHOLE, WHOLE + AHEAD, pass_on, 0)
+
+    @pl.when(outer)
+    def _():
+        lax.fori_loop(WHOLE, steps, pass_on, 0)
+
 
     def self_part():
         contexts = []
@@ -508,64 +551,95 @@
     for k in range(len(others)):
         part_copy(k).start()
 
+    @pl.when(outer)
+    def _():
+        label_copy(mate, 0, 1).wait_recv()
+        label_pass_copy(mate, 1, 1).start()
+
     @pl.when(inner)
     def _():
-        for way in range(3):
-            label_copy(mate, 0, way).wait_recv()
-        sources = [label] + [label_in.at[way] for way in range(3)]
-        nodes = [me, mate, across, beyond]
-        for s, source in enumerate(sources):
+        label_copy(mate, 0, 0).wait_recv()
+        label_pass_copy(across, 0, 4).start()
+
+    def choose(p, ways, nodes):
+        for s, source in enumerate([label] + [label_in.at[way] for way in ways]):
             for c in range(spans):
                 held = jnp.broadcast_to(source[c : c + 1, 0:1], (rows_per, local))
                 for d, node in enumerate(nodes):
                     for l in range(spans):
                         wanted = jnp.full((rows_per, local), node * spans + l, jnp.int32)
-                        pick[s * spans + c, d * spans + l] = jnp.where(
+                        pick[p, s * spans + c, d * spans + l] = jnp.where(
                             held == wanted.astype(jnp.float32), 1.0, 0.0
                         ).astype(jnp.bfloat16)
+
+    def gather(k, p, cross_done, final_done):
+        blocks = [own[k, c] for c in range(spans)]
+        for way in range(3):
+            blocks += [raw_in[way, k, c] for c in range(spans)]
+
+        def gathered(d):
+            total = blocks[0] * pick[p, 0, d]
+            for s in range(1, len(blocks)):
+                total = total + blocks[s] * pick[p, s, d]
+            return total
+
+        for d in range(spans, 2 * spans):
+            cross_out[k, d] = gathered(2 * spans + d)
+        for d in range(spans):
+            cross_out[k, d] = gathered(2 * spans + d)
+        cross_done()
+        for d in range(spans):
+            final_out[k, d] = gathered(spans + d)
+        final_done()
+        for d in range(spans):
+            kept[k, d] = gathered(d)
+
+    def merge_whole(k, _):
+        for way in (1, 2):
+            raw_copy(mate, 0, way, k).wait_recv()
+
+        def cross_done():
+            turn_copy(k).start()
+            cross_copy(k, aside, spans).start()
+
+        gather(k, 1, cross_done, lambda: final_copy(k).start())
+        return 0
+
+    def merge_joined(k, _):
+        for way in range(3):
+            raw_copy(mate, 0, way, k).wait_recv()
+        gather(k, 0, lambda: cross_copy(k, across, 2 * spans).start(), lambda: None)
+        return 0
 
     def merge(k, _):
         for way in range(3):
             raw_copy(mate, 0, way, k).wait_recv()
-        blocks = [own[k, c] for c in range(spans)]
-        for way in range(3):
-            blocks += [raw_in[way, k, c] for c in range(spans)]
-
-        def gathered(d):
-            total = blocks[0] * pick[0, d]
-            for s in range(1, len(blocks)):
-                total = total + blocks[s] * pick[s, d]
-            return total
-
-        for d in range(spans, 2 * spans):
-            cross_out[k, d] = gathered(2 * spans + d)
-        far_copy(k).start()
-        for d in range(spans):
-            cross_out[k, d] = gathered(2 * spans + d)
-        cross_copy(k).start()
-        for d in range(spans):
-            final_out[k, d] = gathered(spans + d)
-        final_copy(k).start()
-        for d in range(spans):
-            kept[k, d] = gathered(d)
-        return 0
-
-    def finish(k, _):
-        cross_copy(k).wait_recv()
+
+        def cross_done():
+            far_copy(k).start()
+            cross_copy(k, across, spans).start()
+
+        gather(k, 0, cross_done, lambda: final_copy(k).start())
+        return 0
+
+    def settle(k):
         a, r = lax.div(k, per), lax.rem(k, per)
         start = pl.multiple_of(r * rows_per, rows_per)
         for l in range(spans):
             moved_cache[a, l, pl.ds(start, rows_per), :] = kept[k, l] + cross_in[k, l]
-        return 0
-
-    def both(k, _):
-        merge(k, 0)
-        finish(k - LAG, 0)
-        return 0
-
-    @pl.when(inner)
-    def _():
-        lax.fori_loop(0, EARLY, merge, 0)
+
+    def finish(k, _):
+        cross_copy(k, across, spans).wait_recv()
+        settle(k)
+        return 0
+
+    def finish_joined(k, _):
+        cross_copy(k, across, 2 * spans).wait_recv()
+        for l in range(spans):
+            final_out[k, l] = final_out[k, l] + cross_in[k, spans + l]
+        final_copy(k).start()
+        settle(k)
+        return 0
 
     loads[1].wait()
     loads[2].wait()
@@ -585,10 +659,6 @@
         normed.astype(jnp.bfloat16), query_proj[...], preferred_element_type=jnp.float32
     ).astype(jnp.bfloat16).astype(jnp.float32)
 
-    @pl.when(inner)
-    def _():
-        lax.fori_loop(EARLY, LAG, merge, 0)
-
     decoded = []
     for c in range(spans):
         mixed = attend(query[c : c + 1], cross[0, c], cross[1, c], None, None)
@@ -599,17 +669,41 @@
     @pl.when(outer)
     def _():
         line_copy(mate, 0, 0).start()
-        line_copy(mate_aside, 1, 1).start()
+        line_copy(aside, 1, 1).start()
 
     @pl.when(inner)
     def _():
         line_copy(aside, 0, 2).start()
 
-    lax.fori_loop(HOLD, steps, pass_on, 0)
+    def turn(k, _):
+        turn_copy(k).wait_recv()
+        turned_copy(k).start()
+        return 0
+
+    def outer_forward(k, _):
+        raw_copy(mate, 0, 0, k).start()
+        raw_copy(mate, 0, 1, k).wait_recv()
+        outer_pass_copy(k).start()
+        return 0
+
+    @pl.when(outer)
+    def _():
+        lax.fori_loop(WHOLE, WHOLE + AHEAD, outer_forward, 0)
+        line_copy(mate, 0, 1).wait_recv()
+        line_pass_copy().start()
+        lax.fori_loop(WHOLE + AHEAD, steps, outer_forward, 0)
+        lax.fori_loop(0, WHOLE, turn, 0)
 
     @pl.when(inner)
     def _():
-        lax.fori_loop(LAG, MIDDLE, both, 0)
+        lax.fori_loop(WHOLE + AHEAD, steps, pass_on, 0)
+
+    def forward(k, _):
+        raw_copy(mate, 0, 0, k).wait_recv()
+        pass_copy(k).start()
+        return 0
+
+    def gather_lines():
         for way in range(3):
             line_copy(mate, 0, way).wait_recv()
         blocks = []
@@ -617,60 +711,145 @@
             blocks += [held[c : c + 1, :].astype(jnp.float32) for c in range(spans)]
         rows = []
         for d in range(4 * spans):
-            total = blocks[0] * pick[0, d, 0:1, :].astype(jnp.float32)
+            total = blocks[0] * pick[0, 0, d, 0:1, :].astype(jnp.float32)
             for s in range(1, len(blocks)):
-                total = total + blocks[s] * pick[s, d, 0:1, :].astype(jnp.float32)
+                total = total + blocks[s] * pick[0, s, d, 0:1, :].astype(jnp.float32)
             rows.append(total)
         line_out[...] = jnp.concatenate(rows[2 * spans :], 0).astype(jnp.bfloat16)
         line_cross_copy().start()
         line_kept[...] = jnp.concatenate(rows[: 2 * spans], 0)
-        lax.fori_loop(MIDDLE, steps, both, 0)
+
+    def send_lines():
         line_cross_copy().wait_recv()
         total = line_kept[...] + line_cross[...].astype(jnp.float32)
         line_last[...] = total[spans:].astype(jnp.bfloat16)
         line_final_copy().start()
         moved_out[...] = total[:spans].astype(jnp.bfloat16)
 
+    def run(groups):
+        while groups:
+            ops, starts = [op for op, _ in groups[0]], [k for _, k in groups[0]]
+            size = 1
+            while size < len(groups) and groups[size] == [(op, k + size) for op, k in groups[0]]:
+                size += 1
+
+            def step(i, _, ops=ops, starts=starts):
+                for op, k in zip(ops, starts):
+                    op(i + k, 0)
+                return 0
+
+            if size > 1:
+                lax.fori_loop(0, size, step, 0)
+            else:
+                step(0, 0)
+            groups = groups[size:]
+
+    def groups(low, high):
+        found = []
+        for k in range(low, high):
+            group = []
+            if k < steps:
+                group.append((merge_joined if k < JOINED else merge, k))
+            if WHOLE <= k - LAG < JOINED:
+                group.append((finish_joined, k - LAG))
+            if k < WHOLE + BEHIND:
+                group.append((merge_whole, k - BEHIND))
+            found.append(group)
+        return found
+
+    @pl.when(inner)
+    def _():
+        lax.fori_loop(0, WHOLE, forward, 0)
+        for way in range(1, 5):
+            label_copy(mate, 0, way).wait_recv()
+        choose(1, (0, 3, 4), (me, mate, aside, mate_aside))
+        choose(0, (0, 1, 2), (me, mate, across, beyond))
+        run([[(merge_whole, k)] for k in range(WHOLE - BEHIND)])
+        run(groups(WHOLE, LINES))
+        gather_lines()
+        run(groups(LINES, steps + LAG))
+        send_lines()
+
+    def place(k, value):
+        a, r = lax.div(k, per), lax.rem(k, per)
+        start = pl.multiple_of(r * rows_per, rows_per)
+        for l in range(spans):
+            moved_cache[a, l, pl.ds(start, rows_per), :] = value(l)
+
     def land(k, _):
         final_copy(k).wait_recv()
         far_copy(k).wait_recv()
-        a, r = lax.div(k, per), lax.rem(k, per)
-        start = pl.multiple_of(r * rows_per, rows_per)
-        for l in range(spans):
-            moved_cache[a, l, pl.ds(start, rows_per), :] = final_in[k, l] + final_far[k, l]
+        place(k, lambda l: final_in[k, l] + final_far[k, l])
+        return 0
+
+    def land_joined(k, _):
+        final_copy(k).wait_recv()
+        place(k, lambda l: final_in[k, l])
         return 0
 
     def outer_sent(k, _):
         raw_copy(mate, 0, 0, k).wait_send()
-        raw_copy(mate_aside, 1, 1, k).wait_send()
+        return 0
+
+    def outer_aside_sent(k, _):
+        raw_copy(aside, 1, 1, k).wait_send()
+        outer_pass_copy(k).wait_send()
+        return 0
+
+    def turned_sent(k, _):
+        turned_copy(k).wait_send()
         return 0
 
     def inner_sent(k, _):
         raw_copy(aside, 0, 2, k).wait_send()
+        final_copy(k).wait_send()
+        return 0
+
+    def cross_sent(k, _):
         far_copy(k).wait_send()
-        cross_copy(k).wait_send()
-        final_copy(k).wait_send()
+        cross_copy(k, across, spans).wait_send()
+        return 0
+
+    def joined_sent(k, _):
+        cross_copy(k, across, 2 * spans).wait_send()
+        return 0
+
+    def pass_sent(k, _):
+        pass_copy(k).wait_send()
         return 0
 
     @pl.when(inner)
     def _():
-        lax.fori_loop(steps - LAG, steps, finish, 0)
+        lax.fori_loop(0, WHOLE, finish, 0)
+        lax.fori_loop(JOINED, steps, finish, 0)
         label_copy(aside, 0, 2).wait_send()
+        label_copy(across, 1, 3).wait_send()
+        label_pass_copy(across, 0, 4).wait_send()
         line_copy(aside, 0, 2).wait_send()
         line_cross_copy().wait_send()
         line_final_copy().wait_send()
         lax.fori_loop(0, steps, inner_sent, 0)
+        lax.fori_loop(0, WHOLE, pass_sent, 0)
+        lax.fori_loop(0, WHOLE, cross_sent, 0)
+        lax.fori_loop(WHOLE, JOINED, joined_sent, 0)
+        lax.fori_loop(JOINED, steps, cross_sent, 0)
 
     @pl.when(outer)
     def _():
-        lax.fori_loop(0, steps, land, 0)
+        lax.fori_loop(0, WHOLE, land, 0)
+        lax.fori_loop(WHOLE, JOINED, land_joined, 0)
+        lax.fori_loop(JOINED, steps, land, 0)
         label_copy(mate, 0, 0).wait_send()
-        label_copy(mate_aside, 1, 1).wait_send()
+        label_copy(aside, 1, 1).wait_send()
+        label_pass_copy(mate, 1, 1).wait_send()
         line_copy(mate, 0, 0).wait_send()
-        line_copy(mate_aside, 1, 1).wait_send()
+        line_copy(aside, 1, 1).wait_send()
+        line_pass_copy().wait_send()
         line_final_copy().wait_recv()
         moved_out[...] = line_final[...]
         lax.fori_loop(0, steps, outer_sent, 0)
+        lax.fori_loop(WHOLE, steps, outer_aside_sent, 0)
+        lax.fori_loop(0, WHOLE, turned_sent, 0)
 
 
 def body(
@@ -729,14 +908,14 @@
             blocks(steps, spans),
             blocks(3, steps, spans),
             blocks(steps, 2 * spans),
+            blocks(steps, 2 * spans),
             blocks(steps, spans),
             blocks(steps, spans),
             blocks(steps, spans),
             blocks(steps, spans),
-            blocks(steps, spans),
-            blocks(4 * spans, 4 * spans),
+            blocks(2, 4 * spans, 4 * spans),
             pltpu.VMEM((8, 128), f32),
-            pltpu.VMEM((3, 8, 128), f32),
+            pltpu.VMEM((5, 8, 128), f32),
             pltpu.VMEM((spans, local), bf16),
             pltpu.VMEM((3, spans, local), bf16),
             pltpu.VMEM((2 * spans, local), f32),
@@ -749,12 +928,13 @@
             dma((2, steps)),
             dma((3, steps)),
             dma((6, steps)),
-            dma((2,)),
             dma((3,)),
-            dma((2,)),
+            dma((5,)),
+            dma((3,)),
             dma((3,)),
             dma((4,)),
             dma((2, cores - 1)),
+            dma((steps,)),
         ]
     else:
         function, specs = kernel, [smem] * 3 + [vmem] * 5

time: 43.1 us -> 39.8 us (0.923)
  Pallas kernels: 40.9 us -> 37.6 us
    pallas_call x1, Pallas kernels: 40.9 us -> 37.6 us  [body(): pl.pallas_call(functools.partial(function, count, cores), out_shape=(pltp...]
where the time goes in v1:
time: 39.8 us; the launch traced here: 39.6 us
  Pallas kernels  37.6 us (94%)
  local copies, waits for them, and re-layouts  1.42 us (4%)
  between operations  0.64 us (2%)
    pallas_call x1, Pallas kernels, body(): pl.pallas_call(functools.partial(function, count, cores), out_shape=(pltp...  37.6 us
    unnamed x2, local copies, waits for them, and re-layouts  1.42 us

profile of v1, /device:TPU:0, one launch (start us, length us, event | category | flops | bytes accessed | tf_op | source)
XLA Modules:
  0.0 39.6 jit_solution(9416279585786694714)
XLA Ops:
  0.6 37.6 %shard_map.122 = (bf16[2,2,128,640]{3,2,1,0:T(8,128)(2,1)S(1)}, bf16[2,640]{1,0:T(2,128)(2,1)S(1)}) custom-call(s32[2]{0:T(128)} %cache_len_hbm.1, s32[2]{0:T(128)} %finished_hbm.1, s32[2]{0:T(128)} %new_slot_hbm.1, bf16[2,1280]{1,0:T(2,128)(2,1)} %hidden_hbm.1, bf16[3,2,640]{2,1,0:T(2,128)(2,1)} %token_qkv_hbm.1, bf16[2,2,128,640]{3,2,1,0:T(8,128)(2,1)} %cache_hbm.1, ...), custom_call_target="tpu_custom_call" | custom-call | tf_op jit(solution)/shard_map/pallas_call | solution.py:956
  38.2 0.8 %copy.15 = bf16[2,2,128,640]{3,2,1,0:T(8,128)(2,1)} copy(bf16[2,2,128,640]{3,2,1,0:T(8,128)(2,1)S(1)} %get-tuple-element.2) | data formatting | bytes 1310720
  39.0 0.6 %copy.16 = bf16[2,640]{1,0:T(2,128)(2,1)} copy(bf16[2,640]{1,0:T(2,128)(2,1)S(1)} %get-tuple-element.3) | data formatting | bytes 5120

commit v2 on v1

--- a/solution.py
+++ b/solution.py
@@ -307,16 +307,19 @@
     part,
     part_in,
     load_sem,
-    raw_send,
-    raw_recv,
-    hop_sems,
+    send_sems,
+    mate_recv,
+    second_recv,
+    whole_recv,
+    cross_recv,
+    final_recv,
+    far_recv,
     label_send,
     label_recv,
     line_send,
     line_recv,
     line_hops,
     part_sems,
-    pass_sems,
 ):
     spans, width = hidden.shape
     slots, local = self_cache.shape[2:]
@@ -339,7 +342,7 @@
     across = (REACH - level) * 2 + column
     beyond = (REACH - mate_level) * 2 + column
     others = [lax.rem(core + k, cores) for k in range(1, cores)]
-    for node in (mate, beyond, aside):
+    for node in (mate, aside):
         greet({"batch": node})
 
     @pl.when(inner)
@@ -384,22 +387,35 @@
             device_id_type=MESH,
         )
 
-    def raw_copy(node, lane, way, k):
-        return to(node, own.at[k], raw_in.at[way, k], raw_send.at[lane, k], raw_recv.at[way, k])
+    own_send, aside_send, pass_send, far_send, cross_send, joined_send, final_send = (
+        send_sems.at[i] for i in range(7)
+    )
+
+    def mate_copy(k):
+        return to(mate, own.at[k], raw_in.at[0, k], own_send, mate_recv.at[k])
+
+    def across_copy(k):
+        return to(across, own.at[k], raw_in.at[1, k], own_send, whole_recv.at[k])
+
+    def aside_copy(k):
+        return to(aside, own.at[k], raw_in.at[2, k], aside_send, second_recv.at[k])
 
     def pass_copy(k):
-        return to(across, raw_in.at[0, k], raw_in.at[2, k], pass_sems.at[k], raw_recv.at[2, k])
+        return to(across, raw_in.at[0, k], raw_in.at[2, k], pass_send, second_recv.at[k])
 
     def outer_pass_copy(k):
-        return to(mate, raw_in.at[1, k], raw_in.at[1, k], pass_sems.at[k], raw_recv.at[1, k])
+        return to(mate, raw_in.at[2, k], raw_in.at[1, k], pass_send, mate_recv.at[k])
+
+    def arrive(blocks, sem):
+        pltpu.make_async_copy(blocks, blocks, sem).wait()
 
     def far_copy(k):
         return to(
             beyond,
             cross_out.at[k, pl.ds(spans, spans)],
             final_far.at[k],
-            hop_sems.at[0, k],
-            hop_sems.at[1, k],
+            far_send,
+            far_recv.at[k - JOINED + WHOLE],
         )
 
     def turn_copy(k):
@@ -407,24 +423,24 @@
             mate,
             cross_out.at[k, pl.ds(spans, spans)],
             raw_in.at[2, k],
-            hop_sems.at[0, k],
-            raw_recv.at[2, k],
+            far_send,
+            second_recv.at[k],
         )
 
     def turned_copy(k):
-        return to(aside, raw_in.at[2, k], final_far.at[k], pass_sems.at[k], hop_sems.at[1, k])
-
-    def cross_copy(k, node, count):
+        return to(aside, raw_in.at[2, k], final_far.at[k], far_send, far_recv.at[k])
+
+    def cross_copy(k, node, count, sent):
         return to(
             node,
             cross_out.at[k, pl.ds(0, count)],
             cross_in.at[k, pl.ds(0, count)],
-            hop_sems.at[2, k],
-            hop_sems.at[3, k],
+            sent,
+            cross_recv.at[k],
         )
 
     def final_copy(k):
-        return to(mate, final_out.at[k], final_in.at[k], hop_sems.at[4, k], hop_sems.at[5, k])
+        return to(mate, final_out.at[k], final_in.at[k], final_send, final_recv.at[k])
 
     def label_copy(node, lane, way):
         return to(node, label, label_in.at[way], label_send.at[lane], label_recv.at[way])
@@ -452,11 +468,11 @@
 
     @pl.when(inner)
     def _():
-        pl.semaphore_wait(barrier, 4 + len(others))
+        pl.semaphore_wait(barrier, 3 + len(others))
 
     @pl.when(outer)
     def _():
-        pl.semaphore_wait(barrier, 3 + len(others))
+        pl.semaphore_wait(barrier, 2 + len(others))
 
     position = lax.broadcasted_iota(jnp.int32, (rows_per, local), 0)
     ends = [cache_len[c] * alive[c] for c in range(spans)]
@@ -480,23 +496,16 @@
 
         @pl.when(outer)
         def _():
-            raw_copy(mate, 0, 0, k).start()
+            mate_copy(k).start()
 
         @pl.when(inner)
         def _():
-            raw_copy(across, 0, 1, k).start()
+            across_copy(k).start()
 
         return 0
 
     def pass_on(k, _):
-        @pl.when(outer)
-        def _():
-            raw_copy(aside, 1, 1, k).start()
-
-        @pl.when(inner)
-        def _():
-            raw_copy(aside, 0, 2, k).start()
-
+        aside_copy(k).start()
         return 0
 
     @pl.when(outer)
@@ -594,30 +603,32 @@
         for d in range(spans):
             kept[k, d] = gathered(d)
 
+    def gathered_in(k):
+        arrive(raw_in.at[pl.ds(0, 2), k], mate_recv.at[k])
+        aside_copy(k).wait_recv()
+
     def merge_whole(k, _):
-        for way in (1, 2):
-            raw_copy(mate, 0, way, k).wait_recv()
+        across_copy(k).wait_recv()
+        pass_copy(k).wait_recv()
 
         def cross_done():
             turn_copy(k).start()
-            cross_copy(k, aside, spans).start()
+            cross_copy(k, aside, spans, cross_send).start()
 
         gather(k, 1, cross_done, lambda: final_copy(k).start())
         return 0
 
     def merge_joined(k, _):
-        for way in range(3):
-            raw_copy(mate, 0, way, k).wait_recv()
-        gather(k, 0, lambda: cross_copy(k, across, 2 * spans).start(), lambda: None)
+        gathered_in(k)
+        gather(k, 0, lambda: cross_copy(k, across, 2 * spans, joined_send).start(), lambda: None)
         return 0
 
     def merge(k, _):
-        for way in range(3):
-            raw_copy(mate, 0, way, k).wait_recv()
+        gathered_in(k)
 
         def cross_done():
             far_copy(k).start()
-            cross_copy(k, across, spans).start()
+            cross_copy(k, across, spans, cross_send).start()
 
         gather(k, 0, cross_done, lambda: final_copy(k).start())
         return 0
@@ -629,12 +640,12 @@
             moved_cache[a, l, pl.ds(start, rows_per), :] = kept[k, l] + cross_in[k, l]
 
     def finish(k, _):
-        cross_copy(k, across, spans).wait_recv()
+        cross_copy(k, across, spans, cross_send).wait_recv()
         settle(k)
         return 0
 
     def finish_joined(k, _):
-        cross_copy(k, across, 2 * spans).wait_recv()
+        cross_copy(k, across, 2 * spans, joined_send).wait_recv()
         for l in range(spans):
             final_out[k, l] = final_out[k, l] + cross_in[k, spans + l]
         final_copy(k).start()
@@ -681,8 +692,8 @@
         return 0
 
     def outer_forward(k, _):
-        raw_copy(mate, 0, 0, k).start()
-        raw_copy(mate, 0, 1, k).wait_recv()
+        mate_copy(k).start()
+        aside_copy(k).wait_recv()
         outer_pass_copy(k).start()
         return 0
 
@@ -699,7 +710,7 @@
         lax.fori_loop(WHOLE + AHEAD, steps, pass_on, 0)
 
     def forward(k, _):
-        raw_copy(mate, 0, 0, k).wait_recv()
+        mate_copy(k).wait_recv()
         pass_copy(k).start()
         return 0
 
@@ -776,6 +787,12 @@
         for l in range(spans):
             moved_cache[a, l, pl.ds(start, rows_per), :] = value(l)
 
+    def land_whole(k, _):
+        final_copy(k).wait_recv()
+        turned_copy(k).wait_recv()
+        place(k, lambda l: final_in[k, l] + final_far[k, l])
+        return 0
+
     def land(k, _):
         final_copy(k).wait_recv()
         far_copy(k).wait_recv()
@@ -787,36 +804,7 @@
         place(k, lambda l: final_in[k, l])
         return 0
 
-    def outer_sent(k, _):
-        raw_copy(mate, 0, 0, k).wait_send()
-        return 0
-
-    def outer_aside_sent(k, _):
-        raw_copy(aside, 1, 1, k).wait_send()
-        outer_pass_copy(k).wait_send()
-        return 0
-
-    def turned_sent(k, _):
-        turned_copy(k).wait_send()
-        return 0
-
-    def inner_sent(k, _):
-        raw_copy(aside, 0, 2, k).wait_send()
-        final_copy(k).wait_send()
-        return 0
-
-    def cross_sent(k, _):
-        far_copy(k).wait_send()
-        cross_copy(k, across, spans).wait_send()
-        return 0
-
-    def joined_sent(k, _):
-        cross_copy(k, across, 2 * spans).wait_send()
-        return 0
-
-    def pass_sent(k, _):
-        pass_copy(k).wait_send()
-        return 0
+    rest, late = steps - WHOLE, steps - JOINED
 
     @pl.when(inner)
     def _():
@@ -828,15 +816,17 @@
         line_copy(aside, 0, 2).wait_send()
         line_cross_copy().wait_send()
         line_final_copy().wait_send()
-        lax.fori_loop(0, steps, inner_sent, 0)
-        lax.fori_loop(0, WHOLE, pass_sent, 0)
-        lax.fori_loop(0, WHOLE, cross_sent, 0)
-        lax.fori_loop(WHOLE, JOINED, joined_sent, 0)
-        lax.fori_loop(JOINED, steps, cross_sent, 0)
+        arrive(own.at[pl.ds(0, WHOLE)], own_send)
+        arrive(own.at[pl.ds(0, rest)], aside_send)
+        arrive(own.at[pl.ds(0, WHOLE)], pass_send)
+        arrive(own.at[pl.ds(0, WHOLE + late)], far_send)
+        arrive(own.at[pl.ds(0, WHOLE + late)], cross_send)
+        arrive(cross_out.at[pl.ds(0, JOINED - WHOLE)], joined_send)
+        arrive(own, final_send)
 
     @pl.when(outer)
     def _():
-        lax.fori_loop(0, WHOLE, land, 0)
+        lax.fori_loop(0, WHOLE, land_whole, 0)
         lax.fori_loop(WHOLE, JOINED, land_joined, 0)
         lax.fori_loop(JOINED, steps, land, 0)
         label_copy(mate, 0, 0).wait_send()
@@ -847,9 +837,10 @@
         line_pass_copy().wait_send()
         line_final_copy().wait_recv()
         moved_out[...] = line_final[...]
-        lax.fori_loop(0, steps, outer_sent, 0)
-        lax.fori_loop(WHOLE, steps, outer_aside_sent, 0)
-        lax.fori_loop(0, WHOLE, turned_sent, 0)
+        arrive(own, own_send)
+        arrive(own.at[pl.ds(0, rest)], aside_send)
+        arrive(own.at[pl.ds(0, rest)], pass_send)
+        arrive(own.at[pl.ds(0, WHOLE)], far_send)
 
 
 def body(
@@ -925,16 +916,19 @@
             pltpu.VMEM((spans, local), bf16),
             *parts,
             dma((12,)),
-            dma((2, steps)),
-            dma((3, steps)),
-            dma((6, steps)),
+            dma((7,)),
+            dma((steps,)),
+            dma((steps,)),
+            dma((WHOLE,)),
+            dma((steps,)),
+            dma((steps,)),
+            dma((WHOLE + steps - JOINED,)),
             dma((3,)),
             dma((5,)),
             dma((3,)),
             dma((3,)),
             dma((4,)),
             dma((2, cores - 1)),
-            dma((steps,)),
         ]
     else:
         function, specs = kernel, [smem] * 3 + [vmem] * 5

time: 39.8 us -> 37.8 us (0.950)
  Pallas kernels: 37.6 us -> 35.6 us
    pallas_call x1, Pallas kernels: 37.6 us -> 35.6 us  [body(): pl.pallas_call(functools.partial(function, count, cores), out_shape=(pltp...]
where the time goes in v2:
time: 37.8 us; the launch traced here: 37.7 us
  Pallas kernels  35.6 us (94%)
  local copies, waits for them, and re-layouts  1.42 us (4%)
  between operations  0.64 us (2%)
    pallas_call x1, Pallas kernels, body(): pl.pallas_call(functools.partial(function, count, cores), out_shape=(pltp...  35.6 us
    unnamed x2, local copies, waits for them, and re-layouts  1.42 us

profile of v2, /device:TPU:0, one launch (start us, length us, event | category | flops | bytes accessed | tf_op | source)
XLA Modules:
  0.0 37.7 jit_solution(555051774162266533)
XLA Ops:
  0.6 35.6 %shard_map.122 = (bf16[2,2,128,640]{3,2,1,0:T(8,128)(2,1)S(1)}, bf16[2,640]{1,0:T(2,128)(2,1)S(1)}) custom-call(s32[2]{0:T(128)} %cache_len_hbm.1, s32[2]{0:T(128)} %finished_hbm.1, s32[2]{0:T(128)} %new_slot_hbm.1, bf16[2,1280]{1,0:T(2,128)(2,1)} %hidden_hbm.1, bf16[3,2,640]{2,1,0:T(2,128)(2,1)} %token_qkv_hbm.1, bf16[2,2,128,640]{3,2,1,0:T(8,128)(2,1)} %cache_hbm.1, ...), custom_call_target="tpu_custom_call" | custom-call | tf_op jit(solution)/shard_map/pallas_call | solution.py:950
  36.3 0.8 %copy.15 = bf16[2,2,128,640]{3,2,1,0:T(8,128)(2,1)} copy(bf16[2,2,128,640]{3,2,1,0:T(8,128)(2,1)S(1)} %get-tuple-element.2) | data formatting | bytes 1310720
  37.1 0.6 %copy.16 = bf16[2,640]{1,0:T(2,128)(2,1)} copy(bf16[2,640]{1,0:T(2,128)(2,1)S(1)} %get-tuple-element.3) | data formatting | bytes 5120

commit v3 on v2

--- a/solution.py
+++ b/solution.py
@@ -13,10 +13,14 @@
 DISTANCES = [3, -3, 2, -2, 1, -1]
 ROWS = 16
 WHOLE = 6
+SPLIT = 12
 JOINED = 14
 AHEAD = 5
 LAG = 3
 BEHIND = 3
+TURNED = 3
+WAIT = 4
+DEFER = 1
 LINES = 11
 
 
@@ -314,12 +318,14 @@
     cross_recv,
     final_recv,
     far_recv,
+    half_recv,
     label_send,
     label_recv,
     line_send,
     line_recv,
     line_hops,
     part_sems,
+    core_sem,
 ):
     spans, width = hidden.shape
     slots, local = self_cache.shape[2:]
@@ -349,8 +355,10 @@
     def _():
         greet({"batch": across})
 
-    for other in others:
-        greet({"mp": other})
+    @pl.when(core == 0)
+    def _():
+        greet({"mp": 1})
+
     loads = [
         pltpu.make_async_copy(source, target, load_sem.at[i])
         for i, (source, target) in enumerate(
@@ -395,7 +403,7 @@
         return to(mate, own.at[k], raw_in.at[0, k], own_send, mate_recv.at[k])
 
     def across_copy(k):
-        return to(across, own.at[k], raw_in.at[1, k], own_send, whole_recv.at[k])
+        return to(across, own.at[k], raw_in.at[1, k], own_send, whole_recv.at[0])
 
     def aside_copy(k):
         return to(aside, own.at[k], raw_in.at[2, k], aside_send, second_recv.at[k])
@@ -415,7 +423,16 @@
             cross_out.at[k, pl.ds(spans, spans)],
             final_far.at[k],
             far_send,
-            far_recv.at[k - JOINED + WHOLE],
+            far_recv.at[k - JOINED + 1],
+        )
+
+    def half_copy(k):
+        return to(
+            across,
+            cross_out.at[k, pl.ds(spans, spans)],
+            cross_in.at[k, pl.ds(spans, spans)],
+            far_send,
+            half_recv.at[k - SPLIT],
         )
 
     def turn_copy(k):
@@ -428,31 +445,34 @@
         )
 
     def turned_copy(k):
-        return to(aside, raw_in.at[2, k], final_far.at[k], far_send, far_recv.at[k])
-
-    def cross_copy(k, node, count, sent):
+        return to(aside, raw_in.at[2, k], final_far.at[k], far_send, far_recv.at[0])
+
+    def cross_copy(k, node, count, sent, slot=None):
         return to(
             node,
             cross_out.at[k, pl.ds(0, count)],
             cross_in.at[k, pl.ds(0, count)],
             sent,
-            cross_recv.at[k],
-        )
-
-    def final_copy(k):
-        return to(mate, final_out.at[k], final_in.at[k], final_send, final_recv.at[k])
+            cross_recv.at[k - TURNED + 1 if slot is None else slot],
+        )
+
+    def final_copy(k, slot):
+        return to(mate, final_out.at[k], final_in.at[k], final_send, final_recv.at[slot])
+
+    def last_copy(k):
+        return final_copy(k, k - SPLIT + 2)
 
     def label_copy(node, lane, way):
-        return to(node, label, label_in.at[way], label_send.at[lane], label_recv.at[way])
+        return to(node, label, label_in.at[way], label_send.at[0], label_recv.at[way])
 
     def line_copy(node, lane, way):
-        return to(node, line, line_in.at[way], line_send.at[lane], line_recv.at[way])
+        return to(node, line, line_in.at[way], line_send.at[0], line_recv.at[way])
 
     def label_pass_copy(node, here, there):
-        return to(node, label_in.at[here], label_in.at[there], label_send.at[2], label_recv.at[there])
+        return to(node, label_in.at[here], label_in.at[there], label_send.at[0], label_recv.at[there])
 
     def line_pass_copy():
-        return to(mate, line_in.at[1], line_in.at[1], line_send.at[2], line_recv.at[1])
+        return to(mate, line_in.at[1], line_in.at[1], line_send.at[0], line_recv.at[1])
 
     def line_cross_copy():
         return to(across, line_out, line_cross, line_hops.at[0], line_hops.at[1])
@@ -468,11 +488,15 @@
 
     @pl.when(inner)
     def _():
-        pl.semaphore_wait(barrier, 3 + len(others))
+        pl.semaphore_wait(barrier, 3 + core)
 
     @pl.when(outer)
     def _():
-        pl.semaphore_wait(barrier, 2 + len(others))
+        pl.semaphore_wait(barrier, 2 + core)
+
+    @pl.when(core == 1)
+    def _():
+        pl.semaphore_signal(core_sem, inc=1, device_id={"mp": 0}, device_id_type=MESH)
 
     position = lax.broadcasted_iota(jnp.int32, (rows_per, local), 0)
     ends = [cache_len[c] * alive[c] for c in range(spans)]
@@ -557,6 +581,11 @@
 
     pad = part.shape[0] - spans
     self_part()
+
+    @pl.when(core == 0)
+    def _():
+        pl.semaphore_wait(core_sem, 1)
+
     for k in range(len(others)):
         part_copy(k).start()
 
@@ -608,29 +637,40 @@
         aside_copy(k).wait_recv()
 
     def merge_whole(k, _):
-        across_copy(k).wait_recv()
         pass_copy(k).wait_recv()
 
         def cross_done():
             turn_copy(k).start()
-            cross_copy(k, aside, spans, cross_send).start()
-
-        gather(k, 1, cross_done, lambda: final_copy(k).start())
-        return 0
+            cross_copy(k, aside, spans, cross_send, 0).start()
+
+        gather(k, 1, cross_done, lambda: final_copy(k, 0).start())
+        return 0
+
+    def merge_whole_joined(k, _):
+        pass_copy(k).wait_recv()
+        gather(k, 1, lambda: cross_copy(k, aside, 2 * spans, joined_send).start(), lambda: None)
+        return 0
+
+    def whole(k):
+        return (merge_whole if k < TURNED else merge_whole_joined, k)
 
     def merge_joined(k, _):
         gathered_in(k)
         gather(k, 0, lambda: cross_copy(k, across, 2 * spans, joined_send).start(), lambda: None)
         return 0
 
+    def merge_half(k, _):
+        gathered_in(k)
+        gather(k, 0, lambda: half_copy(k).start(), lambda: None)
+        return 0
+
     def merge(k, _):
         gathered_in(k)
-
-        def cross_done():
-            far_copy(k).start()
-            cross_copy(k, across, spans, cross_send).start()
-
-        gather(k, 0, cross_done, lambda: final_copy(k).start())
+        gather(k, 0, lambda: far_copy(k).start(), lambda: last_copy(k).start())
+        return 0
+
+    def send_rest(k, _):
+        cross_copy(k, across, spans, cross_send).start()
         return 0
 
     def settle(k):
@@ -644,12 +684,20 @@
         settle(k)
         return 0
 
+    def hand_on(k, copy):
+        for l in range(spans):
+            final_out[k, l] = final_out[k, l] + cross_in[k, spans + l]
+        copy.start()
+
     def finish_joined(k, _):
         cross_copy(k, across, 2 * spans, joined_send).wait_recv()
-        for l in range(spans):
-            final_out[k, l] = final_out[k, l] + cross_in[k, spans + l]
-        final_copy(k).start()
+        hand_on(k, final_copy(k, 1))
         settle(k)
+        return 0
+
+    def finish_half(k, _):
+        half_copy(k).wait_recv()
+        hand_on(k, last_copy(k))
         return 0
 
     loads[1].wait()
@@ -703,7 +751,7 @@
         line_copy(mate, 0, 1).wait_recv()
         line_pass_copy().start()
         lax.fori_loop(WHOLE + AHEAD, steps, outer_forward, 0)
-        lax.fori_loop(0, WHOLE, turn, 0)
+        lax.fori_loop(0, TURNED, turn, 0)
 
     @pl.when(inner)
     def _():
@@ -760,11 +808,19 @@
         for k in range(low, high):
             group = []
             if k < steps:
-                group.append((merge_joined if k < JOINED else merge, k))
+                group.append(
+                    (merge_joined if k < SPLIT else merge_half if k < JOINED else merge, k)
+                )
+            if SPLIT <= k - DEFER < steps and k < steps:
+                group.append((send_rest, k - DEFER))
+            if k == steps - 1:
+                group += [(send_rest, j) for j in range(steps - DEFER, steps)]
             if WHOLE <= k - LAG < JOINED:
-                group.append((finish_joined, k - LAG))
+                group.append((finish_joined if k - LAG < SPLIT else finish_half, k - LAG))
             if k < WHOLE + BEHIND:
-                group.append((merge_whole, k - BEHIND))
+                group.append(whole(k - BEHIND))
+            if TURNED <= k - WHOLE - WAIT + TURNED < WHOLE:
+                group.append((finish_joined, k - WHOLE - WAIT + TURNED))
             found.append(group)
         return found
 
@@ -775,7 +831,8 @@
             label_copy(mate, 0, way).wait_recv()
         choose(1, (0, 3, 4), (me, mate, aside, mate_aside))
         choose(0, (0, 1, 2), (me, mate, across, beyond))
-        run([[(merge_whole, k)] for k in range(WHOLE - BEHIND)])
+        arrive(raw_in.at[1, pl.ds(0, WHOLE)], whole_recv.at[0])
+        run([[whole(k)] for k in range(WHOLE - BEHIND)])
         run(groups(WHOLE, LINES))
         gather_lines()
         run(groups(LINES, steps + LAG))
@@ -787,60 +844,73 @@
         for l in range(spans):
             moved_cache[a, l, pl.ds(start, rows_per), :] = value(l)
 
-    def land_whole(k, _):
-        final_copy(k).wait_recv()
-        turned_copy(k).wait_recv()
+    def land_turned(k, _):
         place(k, lambda l: final_in[k, l] + final_far[k, l])
         return 0
 
+    def land_ready(k, _):
+        place(k, lambda l: final_in[k, l])
+        return 0
+
+    def land_joined(k, _):
+        last_copy(k).wait_recv()
+        return land_ready(k, 0)
+
     def land(k, _):
-        final_copy(k).wait_recv()
+        last_copy(k).wait_recv()
         far_copy(k).wait_recv()
-        place(k, lambda l: final_in[k, l] + final_far[k, l])
-        return 0
-
-    def land_joined(k, _):
-        final_copy(k).wait_recv()
-        place(k, lambda l: final_in[k, l])
-        return 0
-
-    rest, late = steps - WHOLE, steps - JOINED
+        return land_turned(k, 0)
+
+    def settle_turned(k, _):
+        settle(k)
+        return 0
+
+    rest = steps - WHOLE
 
     @pl.when(inner)
     def _():
-        lax.fori_loop(0, WHOLE, finish, 0)
-        lax.fori_loop(JOINED, steps, finish, 0)
-        label_copy(aside, 0, 2).wait_send()
-        label_copy(across, 1, 3).wait_send()
-        label_pass_copy(across, 0, 4).wait_send()
+        arrive(kept.at[pl.ds(0, TURNED)], cross_recv.at[0])
+        lax.fori_loop(0, TURNED, settle_turned, 0)
+        lax.fori_loop(SPLIT, steps, finish, 0)
+        arrive(label_in.at[pl.ds(0, 3)], label_send.at[0])
         line_copy(aside, 0, 2).wait_send()
         line_cross_copy().wait_send()
         line_final_copy().wait_send()
         arrive(own.at[pl.ds(0, WHOLE)], own_send)
         arrive(own.at[pl.ds(0, rest)], aside_send)
         arrive(own.at[pl.ds(0, WHOLE)], pass_send)
-        arrive(own.at[pl.ds(0, WHOLE + late)], far_send)
-        arrive(own.at[pl.ds(0, WHOLE + late)], cross_send)
-        arrive(cross_out.at[pl.ds(0, JOINED - WHOLE)], joined_send)
+        arrive(own.at[pl.ds(0, TURNED + steps - SPLIT)], far_send)
+        arrive(own.at[pl.ds(0, TURNED + steps - SPLIT)], cross_send)
+        arrive(cross_out.at[pl.ds(0, SPLIT - TURNED)], joined_send)
         arrive(own, final_send)
 
     @pl.when(outer)
     def _():
-        lax.fori_loop(0, WHOLE, land_whole, 0)
-        lax.fori_loop(WHOLE, JOINED, land_joined, 0)
+        arrive(final_in.at[pl.ds(0, TURNED)], final_recv.at[0])
+        arrive(final_far.at[pl.ds(0, TURNED)], far_recv.at[0])
+        lax.fori_loop(0, TURNED, land_turned, 0)
+        arrive(final_in.at[pl.ds(TURNED, SPLIT - TURNED)], final_recv.at[1])
+        lax.fori_loop(TURNED, SPLIT, land_ready, 0)
+        lax.fori_loop(SPLIT, JOINED, land_joined, 0)
         lax.fori_loop(JOINED, steps, land, 0)
-        label_copy(mate, 0, 0).wait_send()
-        label_copy(aside, 1, 1).wait_send()
-        label_pass_copy(mate, 1, 1).wait_send()
-        line_copy(mate, 0, 0).wait_send()
-        line_copy(aside, 1, 1).wait_send()
-        line_pass_copy().wait_send()
+        arrive(label_in.at[pl.ds(0, 3)], label_send.at[0])
+        arrive(line_in, line_send.at[0])
         line_final_copy().wait_recv()
         moved_out[...] = line_final[...]
         arrive(own, own_send)
         arrive(own.at[pl.ds(0, rest)], aside_send)
         arrive(own.at[pl.ds(0, rest)], pass_send)
-        arrive(own.at[pl.ds(0, WHOLE)], far_send)
+        arrive(own.at[pl.ds(0, TURNED)], far_send)
+
+
+def store_kernel(cache, out, cache_hbm, out_hbm, sems):
+    copies = [pltpu.make_async_copy(out, out_hbm, sems.at[0])] + [
+        pltpu.make_async_copy(cache.at[a], cache_hbm.at[a], sems.at[1 + a]) for a in range(2)
+    ]
+    for copy in copies:
+        copy.start()
+    for copy in copies:
+        copy.wait()
 
 
 def body(
@@ -883,7 +953,7 @@
     inputs = [pltpu.VMEM(array.shape, bf16) for array in (cross_kv, out_proj, query_proj)]
     parts = [pltpu.VMEM((8, width), f32), pltpu.VMEM((cores - 1, 8, width), f32)]
     steps = 2 * slots // ROWS
-    if count == 2 * (REACH + 1):
+    if count == 2 * (REACH + 1) and cores == 2:
         function, specs = relay_kernel, [away] * 8
 
         def blocks(*lead):
@@ -919,16 +989,18 @@
             dma((7,)),
             dma((steps,)),
             dma((steps,)),
-            dma((WHOLE,)),
-            dma((steps,)),
-            dma((steps,)),
-            dma((WHOLE + steps - JOINED,)),
-            dma((3,)),
+            dma((1,)),
+            dma((steps - TURNED + 1,)),
+            dma((steps - SPLIT + 2,)),
+            dma((steps - JOINED + 1,)),
+            dma((JOINED - SPLIT,)),
+            dma((1,)),
             dma((5,)),
-            dma((3,)),
+            dma((1,)),
             dma((3,)),
             dma((4,)),
             dma((2, cores - 1)),
+            pltpu.SemaphoreType.REGULAR,
         ]
     else:
         function, specs = kernel, [smem] * 3 + [vmem] * 5
@@ -947,7 +1019,7 @@
             dma((2, moves)),
             dma((2, cores - 1)),
         ]
-    return pl.pallas_call(
+    moved = pl.pallas_call(
         functools.partial(function, count, cores),
         out_shape=(
             pltpu.VMEM(self_cache.shape, bf16),
@@ -958,6 +1030,13 @@
         scratch_shapes=scratch,
         compiler_params=pltpu.CompilerParams(collective_id=0, has_side_effects=True),
     )(*operands)
+    return pl.pallas_call(
+        store_kernel,
+        out_shape=tuple(jax.ShapeDtypeStruct(array.shape, bf16) for array in moved),
+        in_specs=[vmem, vmem],
+        out_specs=(away, away),
+        scratch_shapes=[dma((3,))],
+    )(*(pltpu.with_memory_space_constraint(a, pltpu.VMEM) for a in moved))
 
 
 def solution(mesh):

time: 37.8 us -> 37 us (0.979)
  local copies, waits for them, and re-layouts: 1.42 us -> 0 us
  Pallas kernels: 35.6 us -> 36.2 us
    unnamed x2 -> x0, local copies, waits for them, and re-layouts: 1.42 us -> none
    pallas_call x0 -> x1, Pallas kernels: none -> 0.86 us  [body(): pl.pallas_call(store_kernel, out_shape=tuple((jax.ShapeDtypeStruct(array....]
where the time goes in v3:
time: 37 us; the launch traced here: 36.8 us
  Pallas kernels  36.2 us (98%)
  between operations  0.64 us (2%)
    pallas_call x1, Pallas kernels, body(): pl.pallas_call(functools.partial(function, count, cores), out_shape=(pltp...  35.3 us
    pallas_call x1, Pallas kernels, body(): pl.pallas_call(store_kernel, out_shape=tuple((jax.ShapeDtypeStruct(array....  0.86 us

profile of v3, /device:TPU:0, one launch (start us, length us, event | category | flops | bytes accessed | tf_op | source)
XLA Modules:
  0.0 36.8 jit_solution(11155200124323079094)
XLA Ops:
  0.6 35.3 %shard_map.122 = (bf16[2,2,128,640]{3,2,1,0:T(8,128)(2,1)S(1)}, bf16[2,640]{1,0:T(2,128)(2,1)S(1)}) custom-call(s32[2]{0:T(128)} %cache_len_hbm.1, s32[2]{0:T(128)} %finished_hbm.1, s32[2]{0:T(128)} %new_slot_hbm.1, bf16[2,1280]{1,0:T(2,128)(2,1)} %hidden_hbm.1, bf16[3,2,640]{2,1,0:T(2,128)(2,1)} %token_qkv_hbm.1, bf16[2,2,128,640]{3,2,1,0:T(8,128)(2,1)} %cache_hbm.1, ...), custom_call_target="tpu_custom_call" | custom-call | tf_op jit(solution)/shard_map/pallas_call | solution.py:1022
  36.0 0.9 %shard_map.123 = (bf16[2,2,128,640]{3,2,1,0:T(8,128)(2,1)}, bf16[2,640]{1,0:T(2,128)(2,1)}) custom-call(bf16[2,2,128,640]{3,2,1,0:T(8,128)(2,1)S(1)} %get-tuple-element.4.cache, bf16[2,640]{1,0:T(2,128)(2,1)S(1)} %get-tuple-element.5.out), custom_call_target="tpu_custom_call" | custom-call | tf_op jit(solution)/shard_map/pallas_call | solution.py:1033

commit v4 on v3

--- a/solution.py
+++ b/solution.py
@@ -12,16 +12,16 @@
 MESH = pl.DeviceIdType.MESH
 DISTANCES = [3, -3, 2, -2, 1, -1]
 ROWS = 16
-WHOLE = 6
+WHOLE = 7
 SPLIT = 12
 JOINED = 14
 AHEAD = 5
 LAG = 3
 BEHIND = 3
-TURNED = 3
+TURNED = 4
 WAIT = 4
 DEFER = 1
-LINES = 11
+LINES = 12
 
 
 def attend(query, keys, values, length, own):
@@ -550,6 +550,7 @@
 
     @pl.when(inner)
     def _():
+        lax.fori_loop(JOINED, steps, pass_on, 0)
         lax.fori_loop(WHOLE, WHOLE + AHEAD, pass_on, 0)
 
     @pl.when(outer)
@@ -601,14 +602,32 @@
 
     def choose(p, ways, nodes):
         for s, source in enumerate([label] + [label_in.at[way] for way in ways]):
-            for c in range(spans):
-                held = jnp.broadcast_to(source[c : c + 1, 0:1], (rows_per, local))
-                for d, node in enumerate(nodes):
-                    for l in range(spans):
-                        wanted = jnp.full((rows_per, local), node * spans + l, jnp.int32)
-                        pick[p, s * spans + c, d * spans + l] = jnp.where(
-                            held == wanted.astype(jnp.float32), 1.0, 0.0
-                        ).astype(jnp.bfloat16)
+            for d, node in enumerate(nodes):
+                choose_one(p, s, source, d, node)
+
+    def choose_one(p, s, source, d, node):
+        for c in range(spans):
+            held = jnp.broadcast_to(source[c : c + 1, 0:1], (rows_per, local))
+            for l in range(spans):
+                wanted = jnp.full((rows_per, local), node * spans + l, jnp.int32)
+                pick[p, s * spans + c, d * spans + l] = jnp.where(
+                    held == wanted.astype(jnp.float32), 1.0, 0.0
+                ).astype(jnp.bfloat16)
+
+    def level(k, s, d):
+        total = own[k, 0] * pick[0, 0, d]
+        for c in range(1, spans):
+            total = total + own[k, c] * pick[0, c, d]
+        for c in range(spans):
+            total = total + raw_in[2, k, c] * pick[0, s * spans + c, d]
+        return total
+
+    def hand_early(k, _):
+        aside_copy(k).wait_recv()
+        for l in range(spans):
+            final_out[k, l] = level(k, 3, spans + l)
+        last_copy(k).start()
+        return 0
 
     def gather(k, p, cross_done, final_done):
         blocks = [own[k, c] for c in range(spans)]
@@ -626,9 +645,10 @@
         for d in range(spans):
             cross_out[k, d] = gathered(2 * spans + d)
         cross_done()
-        for d in range(spans):
-            final_out[k, d] = gathered(spans + d)
-        final_done()
+        if final_done is not None:
+            for d in range(spans):
+                final_out[k, d] = gathered(spans + d)
+            final_done()
         for d in range(spans):
             kept[k, d] = gathered(d)
 
@@ -665,8 +685,8 @@
         return 0
 
     def merge(k, _):
-        gathered_in(k)
-        gather(k, 0, lambda: far_copy(k).start(), lambda: last_copy(k).start())
+        arrive(raw_in.at[pl.ds(0, 2), k], mate_recv.at[k])
+        gather(k, 0, lambda: far_copy(k).start(), None)
         return 0
 
     def send_rest(k, _):
@@ -755,7 +775,7 @@
 
     @pl.when(inner)
     def _():
-        lax.fori_loop(WHOLE + AHEAD, steps, pass_on, 0)
+        lax.fori_loop(WHOLE + AHEAD, JOINED, pass_on, 0)
 
     def forward(k, _):
         mate_copy(k).wait_recv()
@@ -826,8 +846,12 @@
 
     @pl.when(inner)
     def _():
+        label_copy(mate, 0, 2).wait_recv()
+        choose_one(0, 0, label, 1, mate)
+        choose_one(0, 3, label_in.at[2], 1, mate)
+        lax.fori_loop(JOINED, steps, hand_early, 0)
         lax.fori_loop(0, WHOLE, forward, 0)
-        for way in range(1, 5):
+        for way in (1, 3, 4):
             label_copy(mate, 0, way).wait_recv()
         choose(1, (0, 3, 4), (me, mate, aside, mate_aside))
         choose(0, (0, 1, 2), (me, mate, across, beyond))
@@ -859,7 +883,8 @@
     def land(k, _):
         last_copy(k).wait_recv()
         far_copy(k).wait_recv()
-        return land_turned(k, 0)
+        place(k, lambda l: final_in[k, l] + final_far[k, l] + level(k, 1, l))
+        return 0
 
     def settle_turned(k, _):
         settle(k)
@@ -886,6 +911,8 @@
 
     @pl.when(outer)
     def _():
+        choose_one(0, 0, label, 0, me)
+        choose_one(0, 1, label_in.at[1], 0, me)
         arrive(final_in.at[pl.ds(0, TURNED)], final_recv.at[0])
         arrive(final_far.at[pl.ds(0, TURNED)], far_recv.at[0])
         lax.fori_loop(0, TURNED, land_turned, 0)

time: 37 us -> 36.1 us (0.976)
  Pallas kernels: 36.2 us -> 35.3 us
    pallas_call x1, Pallas kernels: 35.3 us -> 34.5 us  [body(): pl.pallas_call(functools.partial(function, count, cores), out_shape=(pltp...]
where the time goes in v4:
time: 36.1 us; the launch traced here: 36 us
  Pallas kernels  35.3 us (98%)
  between operations  0.64 us (2%)
    pallas_call x1, Pallas kernels, body(): pl.pallas_call(functools.partial(function, count, cores), out_shape=(pltp...  34.5 us
    pallas_call x1, Pallas kernels, body(): pl.pallas_call(store_kernel, out_shape=tuple((jax.ShapeDtypeStruct(array....  0.86 us

profile of v4, /device:TPU:0, one launch (start us, length us, event | category | flops | bytes accessed | tf_op | source)
XLA Modules:
  0.0 36.0 jit_solution(8486309889874163918)
XLA Ops:
  0.6 34.5 %shard_map.122 = (bf16[2,2,128,640]{3,2,1,0:T(8,128)(2,1)S(1)}, bf16[2,640]{1,0:T(2,128)(2,1)S(1)}) custom-call(s32[2]{0:T(128)} %cache_len_hbm.1, s32[2]{0:T(128)} %finished_hbm.1, s32[2]{0:T(128)} %new_slot_hbm.1, bf16[2,1280]{1,0:T(2,128)(2,1)} %hidden_hbm.1, bf16[3,2,640]{2,1,0:T(2,128)(2,1)} %token_qkv_hbm.1, bf16[2,2,128,640]{3,2,1,0:T(8,128)(2,1)} %cache_hbm.1, ...), custom_call_target="tpu_custom_call" | custom-call | tf_op jit(solution)/shard_map/pallas_call | solution.py:1049
  35.1 0.9 %shard_map.123 = (bf16[2,2,128,640]{3,2,1,0:T(8,128)(2,1)}, bf16[2,640]{1,0:T(2,128)(2,1)}) custom-call(bf16[2,2,128,640]{3,2,1,0:T(8,128)(2,1)S(1)} %get-tuple-element.4.cache, bf16[2,640]{1,0:T(2,128)(2,1)S(1)} %get-tuple-element.5.out), custom_call_target="tpu_custom_call" | custom-call | tf_op jit(solution)/shard_map/pallas_call | solution.py:1060

commit v5 on v4

--- a/solution.py
+++ b/solution.py
@@ -13,7 +13,7 @@
 DISTANCES = [3, -3, 2, -2, 1, -1]
 ROWS = 16
 WHOLE = 7
-SPLIT = 12
+SPLIT = 10
 JOINED = 14
 AHEAD = 5
 LAG = 3
@@ -21,7 +21,8 @@
 TURNED = 4
 WAIT = 4
 DEFER = 1
-LINES = 12
+DEFER_ONE = 6
+LINES = 10
 
 
 def attend(query, keys, values, length, own):
@@ -823,7 +824,7 @@
                 step(0, 0)
             groups = groups[size:]
 
-    def groups(low, high):
+    def groups(low, high, defer):
         found = []
         for k in range(low, high):
             group = []
@@ -831,10 +832,10 @@
                 group.append(
                     (merge_joined if k < SPLIT else merge_half if k < JOINED else merge, k)
                 )
-            if SPLIT <= k - DEFER < steps and k < steps:
-                group.append((send_rest, k - DEFER))
+            if SPLIT <= k - defer < steps and k < steps:
+                group.append((send_rest, k - defer))
             if k == steps - 1:
-                group += [(send_rest, j) for j in range(steps - DEFER, steps)]
+                group += [(send_rest, j) for j in range(steps - defer, steps)]
             if WHOLE <= k - LAG < JOINED:
                 group.append((finish_joined if k - LAG < SPLIT else finish_half, k - LAG))
             if k < WHOLE + BEHIND:
@@ -857,9 +858,17 @@
         choose(0, (0, 1, 2), (me, mate, across, beyond))
         arrive(raw_in.at[1, pl.ds(0, WHOLE)], whole_recv.at[0])
         run([[whole(k)] for k in range(WHOLE - BEHIND)])
-        run(groups(WHOLE, LINES))
+        run(groups(WHOLE, LINES, DEFER))
         gather_lines()
-        run(groups(LINES, steps + LAG))
+
+        @pl.when(core == 0)
+        def _():
+            run(groups(LINES, steps + LAG, DEFER))
+
+        @pl.when(core != 0)
+        def _():
+            run(groups(LINES, steps + LAG, DEFER_ONE))
+
         send_lines()
 
     def place(k, value):

time: 36.1 us -> 35.8 us (level)
    pallas_call x1, Pallas kernels: 34.5 us -> 34.1 us  [body(): pl.pallas_call(functools.partial(function, count, cores), out_shape=(pltp...]
where the time goes in v5:
time: 35.8 us; the launch traced here: 35.6 us
  Pallas kernels  35 us (98%)
  between operations  0.64 us (2%)
    pallas_call x1, Pallas kernels, body(): pl.pallas_call(functools.partial(function, count, cores), out_shape=(pltp...  34.1 us
    pallas_call x1, Pallas kernels, body(): pl.pallas_call(store_kernel, out_shape=tuple((jax.ShapeDtypeStruct(array....  0.86 us

profile of v5, /device:TPU:0, one launch (start us, length us, event | category | flops | bytes accessed | tf_op | source)
XLA Modules:
  0.0 35.6 jit_solution(838736526017776528)
XLA Ops:
  0.6 34.1 %shard_map.122 = (bf16[2,2,128,640]{3,2,1,0:T(8,128)(2,1)S(1)}, bf16[2,640]{1,0:T(2,128)(2,1)S(1)}) custom-call(s32[2]{0:T(128)} %cache_len_hbm.1, s32[2]{0:T(128)} %finished_hbm.1, s32[2]{0:T(128)} %new_slot_hbm.1, bf16[2,1280]{1,0:T(2,128)(2,1)} %hidden_hbm.1, bf16[3,2,640]{2,1,0:T(2,128)(2,1)} %token_qkv_hbm.1, bf16[2,2,128,640]{3,2,1,0:T(8,128)(2,1)} %cache_hbm.1, ...), custom_call_target="tpu_custom_call" | custom-call | tf_op jit(solution)/shard_map/pallas_call | solution.py:1058
  34.7 0.9 %shard_map.123 = (bf16[2,2,128,640]{3,2,1,0:T(8,128)(2,1)}, bf16[2,640]{1,0:T(2,128)(2,1)}) custom-call(bf16[2,2,128,640]{3,2,1,0:T(8,128)(2,1)S(1)} %get-tuple-element.4.cache, bf16[2,640]{1,0:T(2,128)(2,1)S(1)} %get-tuple-element.5.out), custom_call_target="tpu_custom_call" | custom-call | tf_op jit(solution)/shard_map/pallas_call | solution.py:1069

commit v6 on v5

--- a/solution.py
+++ b/solution.py
@@ -18,7 +18,7 @@
 AHEAD = 5
 LAG = 3
 BEHIND = 3
-TURNED = 4
+TURNED = 5
 WAIT = 4
 DEFER = 1
 DEFER_ONE = 6

time: 35.8 us -> 35.7 us (level)
  no operation moved by 1% of the time
where the time goes in v6:
time: 35.7 us; the launch traced here: 35.6 us
  Pallas kernels  34.9 us (98%)
  between operations  0.64 us (2%)
    pallas_call x1, Pallas kernels, body(): pl.pallas_call(functools.partial(function, count, cores), out_shape=(pltp...  34.1 us
    pallas_call x1, Pallas kernels, body(): pl.pallas_call(store_kernel, out_shape=tuple((jax.ShapeDtypeStruct(array....  0.86 us

profile of v6, /device:TPU:0, one launch (start us, length us, event | category | flops | bytes accessed | tf_op | source)
XLA Modules:
  0.0 35.6 jit_solution(17267601627924465667)
XLA Ops:
  0.6 34.1 %shard_map.122 = (bf16[2,2,128,640]{3,2,1,0:T(8,128)(2,1)S(1)}, bf16[2,640]{1,0:T(2,128)(2,1)S(1)}) custom-call(s32[2]{0:T(128)} %cache_len_hbm.1, s32[2]{0:T(128)} %finished_hbm.1, s32[2]{0:T(128)} %new_slot_hbm.1, bf16[2,1280]{1,0:T(2,128)(2,1)} %hidden_hbm.1, bf16[3,2,640]{2,1,0:T(2,128)(2,1)} %token_qkv_hbm.1, bf16[2,2,128,640]{3,2,1,0:T(8,128)(2,1)} %cache_hbm.1, ...), custom_call_target="tpu_custom_call" | custom-call | tf_op jit(solution)/shard_map/pallas_call | solution.py:1058
  34.7 0.9 %shard_map.123 = (bf16[2,2,128,640]{3,2,1,0:T(8,128)(2,1)}, bf16[2,640]{1,0:T(2,128)(2,1)}) custom-call(bf16[2,2,128,640]{3,2,1,0:T(8,128)(2,1)S(1)} %get-tuple-element.4.cache, bf16[2,640]{1,0:T(2,128)(2,1)S(1)} %get-tuple-element.5.out), custom_call_target="tpu_custom_call" | custom-call | tf_op jit(solution)/shard_map/pallas_call | solution.py:1069
